TPU v7x, 32 devices: a whole 2x2x4 slice. The times are simulated.
32 devices in a mesh: ga: 2 (over core), band: 16 (over z, y, x).
Axes of the slice: x: 2, y: 2, z: 4, core: 2. Of those that a mesh axis runs over, the one named last changes fastest.
Arguments:
- orbitals: bfloat16 [1024, 2, 16384], P('band', None, 'ga'), may hold values from -6 to 6
- projectors: bfloat16 [864, 2, 16384], P(None, None, ('ga', 'band')), may hold values from -0.03125 to 0.03125
- coupling: float32 [4, 18, 18], replicated, may hold values from -6 to 6
- species: int32 [48], replicated, may hold values from 0 to 3
- offsets: int32 [48], replicated, may hold values from 0 to 846, as said below
Outputs:
- applied: bfloat16 [1024, 2, 16384], P('band', None, 'ga')
Inputs may be any that keep to these rules, and one draw needn't show every extreme that they name: Each atom's 18 projectors are the 18 consecutive rows of projectors starting at its offset; offsets are multiples of 18, and the atoms' blocks are distinct and cover all 864 rows.
All inputs are finite; a program needn't handle non-finite values.
Results may differ from a plain program's by a relative error of at most 0.0049.
Values may be sent and summed in bfloat16 or wider, within the bound.
A program may use at most 64 MiB of HBM per device.

v0:
```python
import jax
import jax.numpy as jnp
from jax import lax
from jax.sharding import PartitionSpec as P


def block_matrices(coupling, species, offsets):
    per_atom = coupling.shape[1]
    count = offsets.shape[0]
    blocks = jnp.arange(count, dtype=jnp.int32)
    matches = (offsets[None, :] == blocks[:, None] * per_atom).astype(jnp.int32)
    atom_kind = jnp.sum(matches * species[None, :], axis=1)
    onehot = (atom_kind[:, None] == jnp.arange(coupling.shape[0], dtype=jnp.int32)[None, :]).astype(
        jnp.float32
    )
    table = coupling.reshape(coupling.shape[0], per_atom * per_atom)
    picked = jnp.dot(
        onehot, table, precision=lax.Precision.HIGHEST, preferred_element_type=jnp.float32
    )
    return picked.reshape(count, per_atom, per_atom)


def apply_coupling(matrices, becp):
    count = matrices.shape[0]
    per_atom = matrices.shape[1]
    height = becp.shape[0]
    widths = becp.shape[2]
    blocked = becp.reshape(count, per_atom, 2 * widths)
    coupled = jnp.einsum("aij,ajc->aic", matrices, blocked, precision=lax.Precision.HIGHEST)
    return coupled.reshape(height, 2, widths).astype(jnp.bfloat16)


def project_bands(projectors, spread):
    total_proj = projectors.shape[0]
    total_bands = spread.shape[0]
    flat_proj = projectors.reshape(total_proj, -1)
    turned = jnp.concatenate([spread[:, 1, :], -spread[:, 0, :]], axis=1)
    stacked = jnp.concatenate([spread.reshape(total_bands, -1), turned], axis=0)
    partial_value = lax.dot_general(
        flat_proj, stacked, (((1,), (1,)), ((), ())), preferred_element_type=jnp.float32
    )
    return partial_value.reshape(total_proj, 2, total_bands)


def add_back(projectors, dbecp):
    total_proj = projectors.shape[0]
    total_bands = dbecp.shape[2]
    columns = dbecp.reshape(total_proj, 2 * total_bands)
    real_part = lax.dot_general(
        columns, projectors[:, 0, :], (((0,), (0,)), ((), ())), preferred_element_type=jnp.float32
    )
    imag_part = lax.dot_general(
        columns, projectors[:, 1, :], (((0,), (0,)), ((), ())), preferred_element_type=jnp.float32
    )
    out_real = real_part[:total_bands] - imag_part[total_bands:]
    out_imag = imag_part[:total_bands] + real_part[total_bands:]
    return jnp.stack([out_real, out_imag], axis=1).astype(jnp.bfloat16)


def per_device(orbitals, projectors, coupling, species, offsets):
    matrices = block_matrices(coupling, species, offsets)
    spread = lax.all_to_all(orbitals, "band", split_axis=2, concat_axis=0, tiled=True)
    partial_value = project_bands(projectors, spread)
    becp = lax.psum(partial_value, ("ga", "band"))
    dbecp = apply_coupling(matrices, becp)
    result = add_back(projectors, dbecp)
    return lax.all_to_all(result, "band", split_axis=0, concat_axis=2, tiled=True)


def solution(mesh):
    placed = (P("band", None, "ga"), P(None, None, ("ga", "band")), P(), P(), P())
    return jax.shard_map(
        per_device, mesh=mesh, in_specs=placed, out_specs=P("band", None, "ga"), check_vma=False
    )
```

profile of v0, /device:TPU:0, one launch (start us, length us, event | category | flops | bytes accessed | tf_op | source)
XLA Modules:
  0.0 417.0 jit_solution(8911082358564989493)
XLA Ops:
  6.5 11.4 %copy.45 = bf16[64,2,8192]{0,1,2:T(2,128)(2,1)} copy(bf16[64,2,8192]{2,1,0:T(2,128)(2,1)} %param.5) | data formatting | bytes 4194304 | tf_op args[0]
  17.9 7.5 %reshape.39 = bf16[16,2,32768]{2,1,0:T(2,128)(2,1)} reshape(bf16[8192,2,64]{2,1,0:T(2,128)(2,1)} %bitcast.46) | data formatting | bytes 4194304
  25.4 0.0 copy-start
  25.4 8.5 %all-to-all-start = ((bf16[16,2,32768]{2,1,0:T(2,128)(2,1)}), bf16[16,2,32768]{2,1,0:T(2,128)(2,1)}, u32[]{:S(2)}, u32[]{:S(2)}) async-start(bf16[16,2,32768]{2,1,0:T(2,128)(2,1)} %reshape.39), calls=%async_computation | async-start | bytes 4194304 | tf_op jit(solution)/shard_map/all_to_all | solution.py:62
  34.0 0.0 all-reduce.2.cloned.1.call-start
  34.0 0.0 copy-done
  34.0 0.5 copy.60
  34.5 42.6 %all-to-all-done = bf16[16,2,32768]{2,1,0:T(2,128)(2,1)} async-done(((bf16[16,2,32768]{2,1,0:T(2,128)(2,1)}), bf16[16,2,32768]{2,1,0:T(2,128)(2,1)}, u32[]{:S(2)}, u32[]{:S(2)}) %all-to-all-start) | async-done | bytes 2097184 | tf_op jit(solution)/shard_map/all_to_all | solution.py:62
  77.1 7.4 %reshape.40 = bf16[8192,2,64]{2,1,0:T(2,128)(2,1)} reshape(bf16[16,2,32768]{2,1,0:T(2,128)(2,1)} %all-to-all-done) | data formatting | bytes 4194304
  84.4 10.6 %copy.55 = bf16[64,2,16,512]{3,0,2,1:T(8,128)(2,1)} copy(bf16[64,2,16,512]{0,1,3,2:T(2,128)(2,1)} %bitcast.44) | data formatting | bytes 4194304 | tf_op jit(solution)/shard_map/all_to_all | solution.py:62
  95.0 7.4 %copy.54 = bf16[64,2,16,512]{3,2,0,1:T(8,128)(2,1)} copy(bf16[64,2,16,512]{0,1,3,2:T(2,128)(2,1)} %bitcast.45) | data formatting | bytes 4194304 | tf_op jit(solution)/shard_map/all_to_all | solution.py:62
  102.4 0.0 copy-start.1
  102.4 1.8 slice_bitcast_fusion
  104.2 0.4 copy-done.1
  104.6 2.2 copy.47
  106.8 0.6 copy.59
  107.4 12.5 %fusion.6 = f32[864,2048]{1,0:T(8,128)} fusion(bf16[864,1024]{1,0:T(8,128)(2,1)S(1)} %bitcast.53, bf16[1024,512]{1,0:T(8,128)(2,1)S(1)} %get-tuple-element.8, bf16[1024,512]{1,0:T(8,128)(2,1)S(1)} %get-tuple-element.7, bf16[1024,1024]{1,0:T(8,128)(2,1)S(1)} %bitcast.52), kind=kOutput, calls=%fused_computation.6 | convolution fusion | flops 3636461568 | bytes 13041664 | tf_op jit(solution)/shard_map/dot_general | solution.py:39
  119.9 7.9 %reshape.36 = f32[48,18,2048]{2,1,0:T(8,128)} reshape(f32[864,2048]{1,0:T(8,128)} %fusion.6) | data formatting | bytes 14155776 | tf_op jit(solution)/shard_map/reshape | solution.py:28
  127.8 0.0 copy-start.5
  127.8 0.0 copy-start.6
  127.8 0.0 copy-start.7
  127.8 0.0 all-reduce.2.cloned.1.call-update
  127.8 0.7 copy-done.5
  128.6 0.1 reshape.32
  128.6 0.1 dot_general.22
  128.8 0.0 copy-done.6
  128.8 0.0 copy-done.7
  128.8 0.2 select_reduce_fusion
  128.9 0.4 fusion.16
  129.4 0.3 copy.49
  129.7 4.2 %fusion.22 = (bf16[864,1,512]{2,1,0:T(2,128)(2,1)}, bf16[864,1,512]{2,1,0:T(2,128)(2,1)}) fusion(bf16[864,2,512]{2,1,0:T(2,128)(2,1)S(1)} %copy-done), kind=kLoop, calls=%fused_computation.30 | loop fusion | bytes 3538944 | tf_op jit(solution)/shard_map/slice | solution.py:53
  133.9 189.5 %all-reduce.2.cloned.1.call-done = f32[48,18,2048]{2,1,0:T(8,128)} async-done(((f32[48,18,2048]{2,1,0:T(8,128)}), f32[48,18,2048]{2,1,0:T(8,128)}) %all-reduce.2.cloned.1.call-update) | async-done | bytes 7077904 | tf_op jit(solution)/shard_map/psum | solution.py:64
  323.4 12.2 %convolution_convert_fusion = bf16[48,18,2048]{2,1,0:T(8,128)(2,1)} fusion(f32[48,18,18]{2,1,0:T(8,128)S(1)} %copy.49, f32[48,18,2048]{2,1,0:T(8,128)} %all-reduce.2.cloned.1.call-done), kind=kOutput, calls=%fused_computation.7 | convolution fusion | flops 383975424 | bytes 10679040 | tf_op jit(solution)/shard_map/aij,ajc->aic/dot_general | solution.py:29
  335.5 0.0 copy-start.4
  335.5 6.2 %convert_element_type.12 = bf16[864,2048]{1,0:T(8,128)(2,1)} reshape(bf16[48,18,2048]{2,1,0:T(8,128)(2,1)} %convolution_convert_fusion) | data formatting | bytes 7077888 | tf_op jit(solution)/shard_map/convert_element_type | solution.py:30
  341.7 0.0 copy-done.4
  341.7 0.0 copy-start.2
  341.7 0.0 copy-start.3
  341.8 4.6 %fusion.14 = f32[2048,512]{1,0:T(8,128)S(1)} fusion(bf16[864,2048]{1,0:T(8,128)(2,1)} %convert_element_type.12, bf16[864,1,512]{2,1,0:T(2,128)(2,1)S(1)} %copy-done.4), kind=kOutput, calls=%fused_computation.19 | convolution fusion | flops 1811939328 | bytes 8617984 | tf_op jit(solution)/shard_map/dot_general | solution.py:52
  346.3 0.0 copy-done.2
  346.4 0.0 copy-done.3
  346.4 2.4 fusion.15
  348.8 1.2 fusion.11
  350.0 0.2 pad_maximum_fusion
  350.2 2.2 copy.52
  352.4 54.2 %all_to_all.36 = bf16[1024,2,512]{2,1,0:T(2,128)(2,1)S(1)} all-to-all(bf16[1024,2,512]{2,1,0:T(2,128)(2,1)S(1)} %copy.52), channel_id=1, replica_groups=mesh['ga'=2,'band'=16] {'band'}, dimensions={0} | all-to-all | bytes 4194304 | tf_op jit(solution)/shard_map/all_to_all | solution.py:67
  406.5 3.6 copy.58
  (2 shorter events, 0.0 us)
Async XLA Ops:
  25.4 8.6 %copy-start = (bf16[864,2,512]{2,1,0:T(2,128)(2,1)S(1)}, bf16[864,2,512]{2,1,0:T(2,128)(2,1)}, u32[]{:S(2)}) copy-start(bf16[864,2,512]{2,1,0:T(2,128)(2,1)} %param.6) | copy-start | bytes 5308420
  25.4 51.6 %all-to-all-start = ((bf16[16,2,32768]{2,1,0:T(2,128)(2,1)}), bf16[16,2,32768]{2,1,0:T(2,128)(2,1)}, u32[]{:S(2)}, u32[]{:S(2)}) async-start(bf16[16,2,32768]{2,1,0:T(2,128)(2,1)} %reshape.39), calls=%async_computation | async-start | bytes 4194304 | tf_op jit(solution)/shard_map/all_to_all | solution.py:62
  34.0 289.4 %all-reduce.2.cloned.1.call-start = ((), (), s32[]{:S(2)}) async-start(), calls=%async_computation.2 | async-start | bytes 18874368 | tf_op jit(solution)/shard_map/psum | solution.py:64
  102.4 2.2 copy-start.1
  127.8 0.8 copy-start.5
  127.8 1.0 copy-start.6
  127.8 1.0 copy-start.7
  335.5 6.2 %copy-start.4 = (bf16[864,1,512]{2,1,0:T(2,128)(2,1)S(1)}, bf16[864,1,512]{2,1,0:T(2,128)(2,1)}, u32[]{:S(2)}) copy-start(bf16[864,1,512]{2,1,0:T(2,128)(2,1)} %get-tuple-element.9) | copy-start | bytes 2654212
  341.7 4.6 %copy-start.2 = (bf16[864,2048]{1,0:T(8,128)(2,1)S(1)}, bf16[864,2048]{1,0:T(8,128)(2,1)}, u32[]{:S(2)}) copy-start(bf16[864,2048]{1,0:T(8,128)(2,1)} %convert_element_type.12) | copy-start | bytes 10616836
  341.7 4.6 %copy-start.3 = (bf16[864,1,512]{2,1,0:T(2,128)(2,1)S(1)}, bf16[864,1,512]{2,1,0:T(2,128)(2,1)}, u32[]{:S(2)}) copy-start(bf16[864,1,512]{2,1,0:T(2,128)(2,1)} %get-tuple-element.10) | copy-start | bytes 2654212
Sparse Core Ops, SparseCore 0:
  127.9 195.3 all-reduce.1
where the time goes:
time: 419 us; the launch traced here: 417 us
  waiting for transfers between devices  232 us (55%)
  local copies, waits for them, and re-layouts  73.2 us (17%)
  blocking collectives  54.2 us (13%)
  matrix products  32 us (8%)
  between operations  13.6 us (3%)
  starting transfers between devices  8.57 us (2%)
    psum x1, waiting for transfers between devices, per_device(): becp = lax.psum(partial_value, ('ga', 'band'))  189 us
    all_to_all x1, blocking collectives, per_device(): lax.all_to_all(result, 'band', split_axis=0, concat_axis=2, tiled=True)  54.2 us
    all_to_all x1, waiting for transfers between devices, per_device(): lax.all_to_all(orbitals, 'band', split_axis=2, concat_axis=0, tiled=True)  42.6 us
    unnamed x22, local copies, waits for them, and re-layouts  28.5 us
    all_to_all x3, local copies, waits for them, and re-layouts, per_device(): lax.all_to_all(orbitals, 'band', split_axis=2, concat_axis=0, tiled=True)  20.1 us
    dot_general x1, matrix products, project_bands(): lax.dot_general(flat_proj, stacked, (((1,), (1,)), ((), ())), preferred_e...  12.5 us
    dot_general x1, matrix products, apply_coupling(): jnp.einsum('aij,ajc->aic', matrices, blocked, precision=lax.Precision.HIG...  12.2 us
    all_to_all x1, starting transfers between devices, per_device(): lax.all_to_all(orbitals, 'band', split_axis=2, concat_axis=0, tiled=True)  8.52 us
  transfers between devices with their start and end apart: 2, of which 2 were waited for; matrix products, arithmetic and copies ran while one was open for 1% of the time, Pallas kernels for 0%

commit v1 on v0

--- a/solution.py
+++ b/solution.py
@@ -59,7 +59,11 @@
 
 def per_device(orbitals, projectors, coupling, species, offsets):
     matrices = block_matrices(coupling, species, offsets)
-    spread = lax.all_to_all(orbitals, "band", split_axis=2, concat_axis=0, tiled=True)
+    w1 = lax.psum(1, axis_name="band")
+    f_next = jnp.split(orbitals, w1, axis=2)
+    found_now = jnp.stack(f_next)
+    x_new = lax.all_to_all(found_now, axis_name="band", split_axis=0, concat_axis=0)
+    spread = jnp.concatenate(x_new, axis=0)
     partial_value = project_bands(projectors, spread)
     becp = lax.psum(partial_value, ("ga", "band"))
     dbecp = apply_coupling(matrices, becp)

time: 419 us -> 394 us (0.940)
  local copies, waits for them, and re-layouts: 73.2 us -> 55 us
    all_to_all x3 -> x1, local copies, waits for them, and re-layouts: 20.1 us -> 0.45 us  [per_device(): lax.all_to_all(found_now, axis_name='band', split_axis=0, concat_axis=0)]
    unnamed x22 -> x30, local copies, waits for them, and re-layouts: 28.5 us -> 30.1 us
  transfers between devices with their start and end apart: 2 -> 2, of which waited for: 2 -> 2; matrix products, arithmetic and copies ran while one was open for 1% -> 2% of each run, Pallas kernels for 0% -> 0%
where the time goes in v1:
time: 394 us
  waiting for transfers between devices  229 us (58%)
  local copies, waits for them, and re-layouts  55 us (14%)
  blocking collectives  54.2 us (14%)
  matrix products  31.5 us (8%)
  between operations  13.6 us (3%)
  starting transfers between devices  8.38 us (2%)
    psum x1, waiting for transfers between devices, per_device(): becp = lax.psum(partial_value, ('ga', 'band'))  189 us
    all_to_all x1, blocking collectives, per_device(): lax.all_to_all(result, 'band', split_axis=0, concat_axis=2, tiled=True)  54.2 us
    all_to_all x1, waiting for transfers between devices, per_device(): lax.all_to_all(found_now, axis_name='band', split_axis=0, concat_axis=0)  39.8 us
    unnamed x30, local copies, waits for them, and re-layouts  30.1 us
    dot_general x1, matrix products, project_bands(): lax.dot_general(flat_proj, stacked, (((1,), (1,)), ((), ())), preferred_e...  12.5 us
    dot_general x1, matrix products, apply_coupling(): jnp.einsum('aij,ajc->aic', matrices, blocked, precision=lax.Precision.HIG...  12.2 us
    all_to_all x1, starting transfers between devices, per_device(): lax.all_to_all(found_now, axis_name='band', split_axis=0, concat_axis=0)  8.34 us
    reshape x1, local copies, waits for them, and re-layouts, apply_coupling(): blocked = becp.reshape(count, per_atom, 2 * widths)  7.92 us
  transfers between devices with their start and end apart: 2, of which 2 were waited for; matrix products, arithmetic and copies ran while one was open for 2% of the time, Pallas kernels for 0%

profile of v1, /device:TPU:0, one launch (start us, length us, event | category | flops | bytes accessed | tf_op | source)
XLA Modules:
  0.0 393.7 jit_solution(9787922111602768360)
XLA Ops:
  6.5 1.6 bitcast_dynamic-update-slice_fusion.15
  8.2 1.6 bitcast_dynamic-update-slice_fusion.14
  9.8 1.6 bitcast_dynamic-update-slice_fusion.13
  11.5 1.6 bitcast_dynamic-update-slice_fusion.12
  13.1 1.6 bitcast_dynamic-update-slice_fusion.11
  14.8 1.6 bitcast_dynamic-update-slice_fusion.10
  16.4 1.6 bitcast_dynamic-update-slice_fusion.9
  18.1 1.6 bitcast_dynamic-update-slice_fusion.8
  19.7 1.6 bitcast_dynamic-update-slice_fusion.7
  21.4 1.6 bitcast_dynamic-update-slice_fusion.6
  23.0 1.6 bitcast_dynamic-update-slice_fusion.5
  24.7 1.6 bitcast_dynamic-update-slice_fusion.4
  26.3 1.6 bitcast_dynamic-update-slice_fusion.3
  28.0 1.6 bitcast_dynamic-update-slice_fusion.2
  29.6 1.6 bitcast_dynamic-update-slice_fusion.1
  31.3 1.6 bitcast_dynamic-update-slice_fusion
  32.9 8.3 %all-to-all-start = ((bf16[16,64,2,512]{3,2,1,0:T(2,128)(2,1)}), bf16[16,64,2,512]{3,2,1,0:T(2,128)(2,1)S(1)}, u32[]{:S(2)}, u32[]{:S(2)}) async-start(bf16[16,64,2,512]{3,2,1,0:T(2,128)(2,1)} %bitcast_dynamic-update-slice_fusion), calls=%async_computation | async-start | bytes 4194304 | tf_op jit(solution)/shard_map/all_to_all | solution.py:65
  41.3 0.0 all-reduce.2.cloned.1.call-start
  41.3 3.2 copy.33
  44.5 39.8 %all-to-all-done = bf16[16,64,2,512]{3,2,1,0:T(2,128)(2,1)S(1)} async-done(((bf16[16,64,2,512]{3,2,1,0:T(2,128)(2,1)}), bf16[16,64,2,512]{3,2,1,0:T(2,128)(2,1)S(1)}, u32[]{:S(2)}, u32[]{:S(2)}) %all-to-all-start) | async-done | bytes 2097184 | tf_op jit(solution)/shard_map/all_to_all | solution.py:65
  84.3 0.4 copy.23
  84.8 0.1 slice_bitcast_fusion
  84.9 0.0 copy-start.2
  84.9 0.6 copy.32
  85.5 0.9 copy-done.2
  86.4 12.5 %fusion.6 = f32[864,2048]{1,0:T(8,128)} fusion(bf16[864,1024]{1,0:T(8,128)(2,1)S(1)} %bitcast.75, bf16[1024,512]{1,0:T(8,128)(2,1)S(1)} %get-tuple-element.8, bf16[1024,512]{1,0:T(8,128)(2,1)S(1)} %get-tuple-element.7, bf16[1024,1024]{1,0:T(8,128)(2,1)S(1)} %bitcast.74), kind=kOutput, calls=%fused_computation.6 | convolution fusion | flops 3636461568 | bytes 13041664 | tf_op jit(solution)/shard_map/dot_general | solution.py:39
  98.9 7.9 %reshape.35 = f32[48,18,2048]{2,1,0:T(8,128)} reshape(f32[864,2048]{1,0:T(8,128)} %fusion.6) | data formatting | bytes 14155776 | tf_op jit(solution)/shard_map/reshape | solution.py:28
  106.8 0.0 copy-start.3
  106.8 0.0 copy-start.4
  106.8 0.0 copy-start.5
  106.8 0.0 copy-start
  106.8 0.0 all-reduce.2.cloned.1.call-update
  106.8 0.7 copy-done.3
  107.6 0.1 reshape.31
  107.7 0.1 dot_general.22
  107.8 0.0 copy-done.4
  107.8 0.0 copy-done.5
  107.8 0.2 select_reduce_fusion
  108.0 0.4 fusion.16
  108.4 0.3 copy.24
  108.7 0.0 copy-done
  108.7 4.2 %fusion.22 = (bf16[864,1,512]{2,1,0:T(2,128)(2,1)}, bf16[864,1,512]{2,1,0:T(2,128)(2,1)}) fusion(bf16[864,2,512]{2,1,0:T(2,128)(2,1)S(1)} %copy-done), kind=kLoop, calls=%fused_computation.46 | loop fusion | bytes 3538944 | tf_op jit(solution)/shard_map/slice | solution.py:53
  112.9 189.5 %all-reduce.2.cloned.1.call-done = f32[48,18,2048]{2,1,0:T(8,128)} async-done(((f32[48,18,2048]{2,1,0:T(8,128)}), f32[48,18,2048]{2,1,0:T(8,128)}) %all-reduce.2.cloned.1.call-update) | async-done | bytes 7077904 | tf_op jit(solution)/shard_map/psum | solution.py:68
  302.4 12.2 %convolution_convert_fusion = bf16[48,18,2048]{2,1,0:T(8,128)(2,1)} fusion(f32[48,18,18]{2,1,0:T(8,128)S(1)} %copy.24, f32[48,18,2048]{2,1,0:T(8,128)} %all-reduce.2.cloned.1.call-done), kind=kOutput, calls=%fused_computation.7 | convolution fusion | flops 383975424 | bytes 10679040 | tf_op jit(solution)/shard_map/aij,ajc->aic/dot_general | solution.py:29
  314.6 4.3 %convert_element_type.12 = bf16[864,2048]{1,0:T(8,128)(2,1)S(1)} reshape(bf16[48,18,2048]{2,1,0:T(8,128)(2,1)} %convolution_convert_fusion) | data formatting | bytes 7077888 | tf_op jit(solution)/shard_map/convert_element_type | solution.py:30
  318.9 0.0 copy-start.1
  318.9 4.0 %fusion.14 = f32[2048,512]{1,0:T(8,128)S(1)} fusion(bf16[864,2048]{1,0:T(8,128)(2,1)S(1)} %convert_element_type.12, bf16[864,1,512]{2,1,0:T(2,128)(2,1)} %get-tuple-element.9), kind=kOutput, calls=%fused_computation.19 | convolution fusion | flops 1811939328 | bytes 8617984 | tf_op jit(solution)/shard_map/dot_general | solution.py:52
  323.0 0.0 copy-done.1
  323.0 2.4 fusion.15
  325.4 1.2 fusion.11
  326.6 0.2 pad_maximum_fusion
  326.8 2.2 copy.27
  329.0 54.2 %all_to_all.23 = bf16[1024,2,512]{2,1,0:T(2,128)(2,1)S(1)} all-to-all(bf16[1024,2,512]{2,1,0:T(2,128)(2,1)S(1)} %copy.27), channel_id=1, replica_groups=mesh['ga'=2,'band'=16] {'band'}, dimensions={0} | all-to-all | bytes 4194304 | tf_op jit(solution)/shard_map/all_to_all | solution.py:71
  383.2 3.6 copy.31
  (2 shorter events, 0.0 us)
Async XLA Ops:
  32.9 51.4 %all-to-all-start = ((bf16[16,64,2,512]{3,2,1,0:T(2,128)(2,1)}), bf16[16,64,2,512]{3,2,1,0:T(2,128)(2,1)S(1)}, u32[]{:S(2)}, u32[]{:S(2)}) async-start(bf16[16,64,2,512]{3,2,1,0:T(2,128)(2,1)} %bitcast_dynamic-update-slice_fusion), calls=%async_computation | async-start | bytes 4194304 | tf_op jit(solution)/shard_map/all_to_all | solution.py:65
  41.3 261.1 %all-reduce.2.cloned.1.call-start = ((), (), s32[]{:S(2)}) async-start(), calls=%async_computation.2 | async-start | bytes 18874368 | tf_op jit(solution)/shard_map/psum | solution.py:68
  84.9 1.5 copy-start.2
  106.8 0.8 copy-start.3
  106.8 1.0 copy-start.4
  106.8 1.0 copy-start.5
  106.8 1.9 copy-start
  318.9 4.1 %copy-start.1 = (bf16[864,1,512]{2,1,0:T(2,128)(2,1)S(1)}, bf16[864,1,512]{2,1,0:T(2,128)(2,1)}, u32[]{:S(2)}) copy-start(bf16[864,1,512]{2,1,0:T(2,128)(2,1)} %get-tuple-element.10) | copy-start | bytes 2654212
Sparse Core Ops, SparseCore 0:
  107.0 195.4 all-reduce.1
